TPU v7x, 128 devices: a whole 4x4x4 slice. The times are simulated.
128 devices in a mesh: section: 32 (over y, z, core), tensor: 4 (over x).
Axes of the slice: x: 4, y: 4, z: 4, core: 2. Of those that a mesh axis runs over, the one named last changes fastest.
Arguments:
- section_input: bfloat16 [32, 512, 4096], P('section', 'tensor'), may hold values from -6 to 6
- history: bfloat16 [32, 7, 512, 4096], P('section', None, 'tensor'), may hold values from -6 to 6
- query_weight: bfloat16 [32, 4096, 3072], P('section', None, 'tensor'), may hold values from -0.4 to 0.4
- key_weight: bfloat16 [32, 4096, 512], P('section', None, 'tensor'), may hold values from -0.4 to 0.4
- value_weight: bfloat16 [32, 4096, 512], P('section', None, 'tensor'), may hold values from -0.09375 to 0.09375
- output_weight: bfloat16 [32, 3072, 4096], P('section', 'tensor'), may hold values from -0.5 to 0.5
- mix_weights: float32 [32, 8], replicated, may hold values from 0.2 to 0.6
Outputs:
- next_input: bfloat16 [32, 512, 4096], P('section', 'tensor')
All inputs are finite; a program needn't handle non-finite values.
Results may differ from a plain program's by a relative error of at most 0.013.
The roundings to bfloat16 on the way count: a program that leaves them out, or rounds other values in their place, can miss the bound.
Values may be sent and summed in bfloat16 or wider, within the bound.
No kernel may reach another device: no remote copies, remote signals or barrier semaphores. Data moves between devices by JAX's collectives and lax.ppermute only.
A program may use at most 128 MiB of HBM per device.

v0:
```python
import math
import jax
import jax.numpy as jnp
from jax import lax
from jax.sharding import PartitionSpec as P

HEAD_DIM = 64
DILATION_STRIDE = 4


def passed_along(value, axis, steps):
    count = lax.axis_size(axis)
    first, last = (max(0, -steps), min(count, count - steps))
    return lax.ppermute(value, axis, [(source, source + steps) for source in range(first, last)])


def from_behind(block, axis, distance):
    devices = range(lax.axis_size(axis))
    route = [((i - distance) % len(devices), i) for i in devices]
    return lax.ppermute(block, axis, route)


def normalize(token_rows):
    values = token_rows.astype(jnp.float32)
    inv_scale = lax.rsqrt(jnp.mean(values * values, axis=-1, keepdims=True) + 1e-05)
    return (values * inv_scale).astype(jnp.bfloat16)


def table_row(table, wanted):
    one_hot = (jnp.arange(table.shape[0], dtype=jnp.int32) == wanted).astype(jnp.float32)
    return jnp.sum(one_hot[:, None] * table, axis=0)


def attend(query_rows, key_rows, value_rows, first_row):
    scores = jnp.einsum(
        "tgjd,sgd->gjts", query_rows, key_rows, preferred_element_type=jnp.float32
    ) / math.sqrt(HEAD_DIM)
    row_positions = first_row + jnp.arange(query_rows.shape[0], dtype=jnp.int32)
    key_positions = jnp.arange(key_rows.shape[0], dtype=jnp.int32)
    scores = jnp.where(row_positions[:, None] >= key_positions[None, :], scores, -1e30)
    softmax_weights = jax.nn.softmax(scores, axis=-1).astype(jnp.bfloat16)
    heads_out = jnp.einsum(
        "gjts,sgd->tgjd", softmax_weights, value_rows, preferred_element_type=jnp.float32
    )
    return heads_out.astype(jnp.bfloat16)


def on_device(
    section_input, history, query_weight, key_weight, value_weight, output_weight, mix_weights
):
    token_rows = section_input[0]
    current_section = lax.axis_index("section")
    slots = history.shape[1]
    self_coefficient = table_row(mix_weights, current_section)
    history_sum = jnp.zeros(token_rows.shape, jnp.float32)
    for history_slot in range(1, slots + 1):
        received_block = passed_along(
            history[0, history_slot - 1], "section", DILATION_STRIDE * history_slot
        )
        factor = jnp.where(
            current_section >= DILATION_STRIDE * history_slot,
            self_coefficient[history_slot],
            jnp.float32(0.0),
        )
        history_sum = history_sum + factor * received_block.astype(jnp.float32)
    normed = normalize(token_rows)
    query_local = query_weight[0]
    key_local = key_weight[0]
    value_local = value_weight[0]
    row_piece = lax.all_gather(normed, "tensor", axis=0, tiled=True)
    query_part = jnp.dot(row_piece, query_local, preferred_element_type=jnp.float32).astype(
        jnp.bfloat16
    )
    key_part = jnp.dot(row_piece, key_local, preferred_element_type=jnp.float32).astype(
        jnp.bfloat16
    )
    value_part = jnp.dot(row_piece, value_local, preferred_element_type=jnp.float32).astype(
        jnp.bfloat16
    )
    projected = jnp.concatenate([query_part, key_part, value_part], axis=1)
    query_width = query_local.shape[1]
    kv_width = key_local.shape[1]
    seq_len = projected.shape[0]
    groups = kv_width // HEAD_DIM
    per_group = query_width // kv_width
    query_rows = projected[:, :query_width].reshape(seq_len, groups, per_group, HEAD_DIM)
    key_rows = projected[:, query_width : query_width + kv_width].reshape(seq_len, groups, HEAD_DIM)
    value_rows = projected[:, query_width + kv_width :].reshape(seq_len, groups, HEAD_DIM)
    block_rows = 512
    block_count = seq_len // block_rows
    blocked = query_rows.reshape(block_count, block_rows, groups, per_group, HEAD_DIM)
    starts = jnp.arange(block_count, dtype=jnp.int32) * block_rows
    attended = lax.map(
        lambda paired: attend(paired[0], key_rows, value_rows, paired[1]), (blocked, starts)
    )
    heads_out = attended.reshape(seq_len, query_width)
    output_local = output_weight[0]
    row_piece = heads_out
    partial_term = jnp.dot(row_piece, output_local, preferred_element_type=jnp.float32).astype(
        jnp.bfloat16
    )
    attention_sum = lax.psum_scatter(
        lax.optimization_barrier(partial_term).astype(jnp.float32).astype(jnp.bfloat16),
        "tensor",
        scatter_dimension=0,
        tiled=True,
    ).astype(jnp.float32)
    block_out = (token_rows.astype(jnp.float32) + attention_sum).astype(jnp.bfloat16)
    mixed = (self_coefficient[0] * block_out.astype(jnp.float32) + history_sum).astype(jnp.bfloat16)
    forwarded = from_behind(mixed, "section", 1)
    return forwarded[None]


def solution(mesh):
    placed = (
        P("section", "tensor", None),
        P("section", None, "tensor", None),
        P("section", None, "tensor"),
        P("section", None, "tensor"),
        P("section", None, "tensor"),
        P("section", "tensor", None),
        P(),
    )
    return jax.shard_map(
        on_device,
        mesh=mesh,
        in_specs=placed,
        out_specs=P("section", "tensor", None),
        check_vma=False,
    )
```

profile of v0, /device:TPU:0, one launch (start us, length us, event | category | flops | bytes accessed | tf_op | source)
XLA Modules:
  0.0 245.2 jit_solution(5167761586907813160)
XLA Ops:
  6.5 1.6 fusion.13
  8.2 2.5 %fusion.14 = bf16[128,4096]{1,0:T(8,128)(2,1)} fusion(bf16[1,128,4096]{2,1,0:T(8,128)(2,1)} %param.7, f32[128]{0:T(128)S(1)} %add_rsqrt_fusion), kind=kLoop, calls=%fused_computation.18 | loop fusion | flops 1572864 | bytes 2097664 | tf_op jit(solution)/shard_map/convert_element_type | solution.py:26
  10.6 0.0 all-gather.2.cloned.1.call-update
  10.6 0.0 reduce-scatter.2.cloned.1.call-start
  10.7 0.1 iota_compare_fusion
  10.8 50.7 %all-gather.2.cloned.1.call-done = bf16[512,4096]{1,0:T(8,128)(2,1)} async-done(((bf16[128,4096]{1,0:T(8,128)(2,1)}), bf16[512,4096]{1,0:T(8,128)(2,1)}) %all-gather.2.cloned.1.call-update) | async-done | bytes 4194320 | tf_op jit(solution)/shard_map/all_gather | solution.py:70
  61.5 7.5 %fusion.19 = bf16[512,768]{1,0:T(8,128)(2,1)S(1)} fusion(bf16[512,4096]{1,0:T(8,128)(2,1)} %all-gather.2.cloned.1.call-done, bf16[1,4096,768]{2,1,0:T(8,128)(2,1)} %param.9), kind=kOutput, calls=%fused_computation.23 | convolution fusion | flops 3221618688 | bytes 11272192 | tf_op jit(solution)/shard_map/dot_general | solution.py:71
  68.9 0.3 copy.10
  69.2 3.7 %convolution_convert_fusion = bf16[512,128]{0,1:T(8,128)(2,1)S(1)} fusion(bf16[512,4096]{1,0:T(8,128)(2,1)} %all-gather.2.cloned.1.call-done, bf16[1,4096,128]{2,1,0:T(8,128)(2,1)S(1)} %copy-done), kind=kOutput, calls=%fused_computation.24 | convolution fusion | flops 536936448 | bytes 5373952 | tf_op jit(solution)/shard_map/dot_general | solution.py:74
  72.9 7.3 %fusion.27 = (f32[2,6,512]{2,1,0:T(8,128)S(1)}, f32[2,6,512,512]{2,3,1,0:T(8,128)}) fusion(pred[512,512]{0,1:T(8,128)(4,1)S(1)} %iota_compare_fusion, bf16[512,2,64,1]{0,2,3,1:T(8,128)(2,1)S(1)} %bitcast.80, bf16[512,2,6,64]{0,3,2,1:T(8,128)(2,1)S(1)} %bitcast.79), kind=kOutput, calls=%fused_computation.42 | convolution fusion | flops 415236608 | bytes 13787136 | tf_op jit(solution)/shard_map/while/body/eval_jaxpr/sub | solution.py:41
  80.2 3.8 %convolution_convert_fusion.1 = bf16[512,128]{0,1:T(8,128)(2,1)S(1)} fusion(bf16[512,4096]{1,0:T(8,128)(2,1)} %all-gather.2.cloned.1.call-done, bf16[1,4096,128]{2,1,0:T(8,128)(2,1)S(1)} %copy-done.2), kind=kOutput, calls=%fused_computation.25 | convolution fusion | flops 536936448 | bytes 5373952 | tf_op jit(solution)/shard_map/dot_general | solution.py:77
  84.1 0.0 slice-start.1
  84.1 6.0 %fusion.18 = bf16[2,64,6,512]{3,1,2,0:T(8,128)(2,1)S(1)} fusion(bf16[512,2,64,1]{0,2,3,1:T(8,128)(2,1)S(1)} %bitcast.81, f32[2,6,512,512]{2,3,1,0:T(8,128)} %get-tuple-element.36, f32[2,6,512]{2,1,0:T(8,128)S(1)} %get-tuple-element.35), kind=kOutput, calls=%fused_computation.22 | convolution fusion | flops 409337856 | bytes 13524992 | tf_op jit(solution)/shard_map/while/body/eval_jaxpr/gjts,sgd->tgjd/dot_general | solution.py:42
  90.1 5.2 %fusion.10 = bf16[512,4096]{1,0:T(8,128)(2,1)} fusion(bf16[512,768]{0,1:T(8,128)(2,1)S(1)} %bitcast.84, bf16[1,768,4096]{2,1,0:T(8,128)(2,1)S(1)} %bitcast.83), kind=kOutput, calls=%fused_computation.13 | convolution fusion | flops 3223322624 | bytes 11272192 | tf_op jit(solution)/shard_map/dot_general | solution.py:99
  95.3 0.0 reduce-scatter.2.cloned.1.call-update
  95.4 5.6 %slice_bitcast_fusion.6 = (bf16[128,4096]{1,0:T(8,128)(2,1)S(1)}, bf16[128,4096]{1,0:T(8,128)(2,1)}, bf16[128,4096]{1,0:T(8,128)(2,1)}, bf16[128,4096]{1,0:T(8,1...) fusion(bf16[1,7,128,4096]{3,2,1,0:T(8,128)(2,1)} %param.8), kind=kLoop, calls=%fused_computation.34 | loop fusion | bytes 14680064 | tf_op jit(solution)/shard_map/squeeze | solution.py:58
  100.9 5.1 %collective-permute-start = (bf16[128,4096]{1,0:T(8,128)(2,1)S(1)}, bf16[128,4096]{1,0:T(8,128)(2,1)S(1)}, u32[]{:S(2)}, u32[]{:S(2)}) collective-permute-start(bf16[128,4096]{1,0:T(8,128)(2,1)S(1)} %get-tuple-element.13), channel_id=1, source_target_pairs={{0,16},{4,20},{8,24},{12,28},{16,32},{20,36},{24,40},{28,44},{32,4... | collective-permute-start | bytes 3145736 | tf_op jit(solution)/shard_map/ppermute | solution.py:14
  106.1 3.4 %collective-permute-start.1 = (bf16[128,4096]{1,0:T(8,128)(2,1)S(1)}, bf16[128,4096]{1,0:T(8,128)(2,1)S(1)}, u32[]{:S(2)}, u32[]{:S(2)}) collective-permute-start(bf16[128,4096]{1,0:T(8,128)(2,1)S(1)} %get-tuple-element.24), channel_id=1, source_target_pairs={{0,32},{4,36},{8,40},{12,44},{16,48},{20,52},{24,56},{28,60},{32,6... | collective-permute-start | bytes 3145736 | tf_op jit(solution)/shard_map/ppermute | solution.py:14
  109.5 4.7 %collective-permute-start.2 = (bf16[128,4096]{1,0:T(8,128)(2,1)}, bf16[128,4096]{1,0:T(8,128)(2,1)}, u32[]{:S(2)}, u32[]{:S(2)}) collective-permute-start(bf16[128,4096]{1,0:T(8,128)(2,1)} %get-tuple-element.22), channel_id=1, source_target_pairs={{0,48},{4,52},{8,56},{12,60},{16,64},{20,68},{24,72},{28,76},{32,8... | collective-permute-start | bytes 3145736 | tf_op jit(solution)/shard_map/ppermute | solution.py:14
  114.2 2.8 %collective-permute-start.3 = (bf16[128,4096]{1,0:T(8,128)(2,1)}, bf16[128,4096]{1,0:T(8,128)(2,1)}, u32[]{:S(2)}, u32[]{:S(2)}) collective-permute-start(bf16[128,4096]{1,0:T(8,128)(2,1)} %get-tuple-element.20), channel_id=1, source_target_pairs={{0,64},{4,68},{8,72},{12,76},{16,80},{20,84},{24,88},{28,92},{32,9... | collective-permute-start | bytes 3145736 | tf_op jit(solution)/shard_map/ppermute | solution.py:14
  117.0 2.3 collective-permute-start.4
  119.3 8.9 %collective-permute-done = bf16[128,4096]{1,0:T(8,128)(2,1)S(1)} collective-permute-done((bf16[128,4096]{1,0:T(8,128)(2,1)S(1)}, bf16[128,4096]{1,0:T(8,128)(2,1)S(1)}, u32[]{:S(2)}, u32[]{:S(2)}) %collective-permute-start) | collective-permute-done | bytes 1048608 | tf_op jit(solution)/shard_map/ppermute | solution.py:14
  128.2 29.9 %collective-permute-start.5 = (bf16[128,4096]{1,0:T(8,128)(2,1)}, bf16[128,4096]{1,0:T(8,128)(2,1)}, u32[]{:S(2)}, u32[]{:S(2)}) collective-permute-start(bf16[128,4096]{1,0:T(8,128)(2,1)} %get-tuple-element.26), channel_id=1, source_target_pairs={{0,96},{4,100},{8,104},{12,108},{16,112},{20,116},{24,120},{28,124... | collective-permute-start | bytes 3145736 | tf_op jit(solution)/shard_map/ppermute | solution.py:14
  158.2 20.5 %collective-permute-start.6 = (bf16[128,4096]{1,0:T(8,128)(2,1)S(1)}, bf16[128,4096]{1,0:T(8,128)(2,1)}, u32[]{:S(2)}, u32[]{:S(2)}) collective-permute-start(bf16[128,4096]{1,0:T(8,128)(2,1)S(1)} %get-tuple-element.25), channel_id=1, source_target_pairs={{0,112},{4,116},{8,120},{12,124},{1,113},{5,117},{9,121},{13,125},... | collective-permute-start | bytes 3145736 | tf_op jit(solution)/shard_map/ppermute | solution.py:14
  178.7 0.1 multiply_reduce_fusion
  178.8 0.7 fusion.26
  183.8 15.1 %collective-permute-done.4 = bf16[128,4096]{1,0:T(8,128)(2,1)} collective-permute-done((bf16[128,4096]{1,0:T(8,128)(2,1)}, bf16[128,4096]{1,0:T(8,128)(2,1)}, u32[]{:S(2)}, u32[]{:S(2)}) %collective-permute-start.4) | collective-permute-done | bytes 1048608 | tf_op jit(solution)/shard_map/ppermute | solution.py:14
  198.9 11.4 %collective-permute-done.6 = bf16[128,4096]{1,0:T(8,128)(2,1)} collective-permute-done((bf16[128,4096]{1,0:T(8,128)(2,1)S(1)}, bf16[128,4096]{1,0:T(8,128)(2,1)}, u32[]{:S(2)}, u32[]{:S(2)}) %collective-permute-start.6) | collective-permute-done | bytes 1048608 | tf_op jit(solution)/shard_map/ppermute | solution.py:14
  210.3 5.8 %add_convert_fusion = bf16[128,4096]{1,0:T(8,128)(2,1)S(1)} fusion(bf16[128,4096]{1,0:T(8,128)(2,1)} %collective-permute-done.6, bf16[128,4096]{1,0:T(8,128)(2,1)} %collective-permute-done.5, bf16[128,4096]{1,0:T(8,128)(2,1)} %collective-permute-done.4, bf16[128,4096]{1,0:T(8,128)(2,1)} %collective-permute-done.3, ...), kind=kLoop, calls=%fused_computation.20 | loop fusion | flops 14680064 | bytes 10485792 | tf_op jit(solution)/shard_map/convert_element_type | solution.py:109
  216.1 0.1 collective-permute-start.7
  216.2 21.2 %collective-permute-done.7 = bf16[128,4096]{1,0:T(8,128)(2,1)S(1)} collective-permute-done((bf16[128,4096]{1,0:T(8,128)(2,1)S(1)}, bf16[128,4096]{1,0:T(8,128)(2,1)S(1)}, u32[]{:S(2)}, u32[]{:S(2)}) %collective-permute-start.7) | collective-permute-done | bytes 1048608 | tf_op jit(solution)/shard_map/ppermute | solution.py:20
  237.4 1.0 copy.16
  (24 shorter events, 0.1 us)
Async XLA Ops:
  6.5 62.7 %copy-start = (bf16[1,4096,128]{2,1,0:T(8,128)(2,1)S(1)}, bf16[1,4096,128]{2,1,0:T(8,128)(2,1)}, u32[]{:S(2)}) copy-start(bf16[1,4096,128]{2,1,0:T(8,128)(2,1)} %param.10) | copy-start | bytes 3145732
  6.5 54.9 %all-gather.2.cloned.1.call-start = ((), (), s32[]{:S(2)}) async-start(), calls=%async_computation.1 | async-start | bytes 5242880 | tf_op jit(solution)/shard_map/all_gather | solution.py:70
  10.6 199.6 %reduce-scatter.2.cloned.1.call-start = ((), (), s32[]{:S(2)}) async-start(), calls=%async_computation.2 | async-start | bytes 5242880 | tf_op jit(solution)/shard_map/reduce_scatter | solution.py:102
  72.9 7.3 %copy-start.2 = (bf16[1,4096,128]{2,1,0:T(8,128)(2,1)S(1)}, bf16[1,4096,128]{2,1,0:T(8,128)(2,1)}, u32[]{:S(2)}) copy-start(bf16[1,4096,128]{2,1,0:T(8,128)(2,1)} %param.11) | copy-start | bytes 3145732
  80.2 9.9 %slice-start = ((s8[6291456]{0:T(1024)(128)(4,1)}), s8[4194304]{0:T(1024)(128)(4,1)S(1)}, s32[]{:S(2)}) async-start(s8[6291456]{0:T(1024)(128)(4,1)} %bitcast.82), calls=%async_computation.3 | async-start | bytes 8388608
  84.1 6.0 %slice-start.1 = ((s8[6291456]{0:T(1024)(128)(4,1)}), s8[2097152]{0:T(1024)(128)(4,1)S(1)}, s32[]{:S(2)}) async-start(s8[6291456]{0:T(1024)(128)(4,1)} %bitcast.82), calls=%async_computation.4 | async-start | bytes 4194304
  95.3 83.4 %copy-start.5 = (f32[32,8]{0,1:T(8,128)S(1)}, f32[32,8]{0,1:T(8,128)}, u32[]{:S(2)}) copy-start(f32[32,8]{0,1:T(8,128)} %param.13) | copy-start | bytes 3076
  95.3 114.9 %copy-start.1 = (bf16[1,128,4096]{2,1,0:T(8,128)(2,1)S(1)}, bf16[1,128,4096]{2,1,0:T(8,128)(2,1)}, u32[]{:S(2)}) copy-start(bf16[1,128,4096]{2,1,0:T(8,128)(2,1)} %param.7) | copy-start | bytes 3145732
  100.9 27.3 %collective-permute-start = (bf16[128,4096]{1,0:T(8,128)(2,1)S(1)}, bf16[128,4096]{1,0:T(8,128)(2,1)S(1)}, u32[]{:S(2)}, u32[]{:S(2)}) collective-permute-start(bf16[128,4096]{1,0:T(8,128)(2,1)S(1)} %get-tuple-element.13), channel_id=1, source_target_pairs={{0,16},{4,20},{8,24},{12,28},{16,32},{20,36},{24,40},{28,44},{32,4... | collective-permute-start | bytes 3145736 | tf_op jit(solution)/shard_map/ppermute | solution.py:14
  106.1 52.1 %collective-permute-start.1 = (bf16[128,4096]{1,0:T(8,128)(2,1)S(1)}, bf16[128,4096]{1,0:T(8,128)(2,1)S(1)}, u32[]{:S(2)}, u32[]{:S(2)}) collective-permute-start(bf16[128,4096]{1,0:T(8,128)(2,1)S(1)} %get-tuple-element.24), channel_id=1, source_target_pairs={{0,32},{4,36},{8,40},{12,44},{16,48},{20,52},{24,56},{28,60},{32,6... | collective-permute-start | bytes 3145736 | tf_op jit(solution)/shard_map/ppermute | solution.py:14
  109.5 74.3 %collective-permute-start.2 = (bf16[128,4096]{1,0:T(8,128)(2,1)}, bf16[128,4096]{1,0:T(8,128)(2,1)}, u32[]{:S(2)}, u32[]{:S(2)}) collective-permute-start(bf16[128,4096]{1,0:T(8,128)(2,1)} %get-tuple-element.22), channel_id=1, source_target_pairs={{0,48},{4,52},{8,56},{12,60},{16,64},{20,68},{24,72},{28,76},{32,8... | collective-permute-start | bytes 3145736 | tf_op jit(solution)/shard_map/ppermute | solution.py:14
  114.2 69.6 %collective-permute-start.3 = (bf16[128,4096]{1,0:T(8,128)(2,1)}, bf16[128,4096]{1,0:T(8,128)(2,1)}, u32[]{:S(2)}, u32[]{:S(2)}) collective-permute-start(bf16[128,4096]{1,0:T(8,128)(2,1)} %get-tuple-element.20), channel_id=1, source_target_pairs={{0,64},{4,68},{8,72},{12,76},{16,80},{20,84},{24,88},{28,92},{32,9... | collective-permute-start | bytes 3145736 | tf_op jit(solution)/shard_map/ppermute | solution.py:14
  117.0 81.9 %collective-permute-start.4 = (bf16[128,4096]{1,0:T(8,128)(2,1)}, bf16[128,4096]{1,0:T(8,128)(2,1)}, u32[]{:S(2)}, u32[]{:S(2)}) collective-permute-start(bf16[128,4096]{1,0:T(8,128)(2,1)} %get-tuple-element.14), channel_id=1, source_target_pairs={{0,80},{4,84},{8,88},{12,92},{16,96},{20,100},{24,104},{28,108},{3... | collective-permute-start | bytes 3145736 | tf_op jit(solution)/shard_map/ppermute | solution.py:14
  128.2 50.5 %copy-start.3 = (bf16[128,4096]{1,0:T(8,128)(2,1)}, bf16[128,4096]{1,0:T(8,128)(2,1)S(1)}, u32[]{:S(2)}) copy-start(bf16[128,4096]{1,0:T(8,128)(2,1)S(1)} %collective-permute-done) | copy-start | bytes 3145732
  128.2 70.7 %collective-permute-start.5 = (bf16[128,4096]{1,0:T(8,128)(2,1)}, bf16[128,4096]{1,0:T(8,128)(2,1)}, u32[]{:S(2)}, u32[]{:S(2)}) collective-permute-start(bf16[128,4096]{1,0:T(8,128)(2,1)} %get-tuple-element.26), channel_id=1, source_target_pairs={{0,96},{4,100},{8,104},{12,108},{16,112},{20,116},{24,120},{28,124... | collective-permute-start | bytes 3145736 | tf_op jit(solution)/shard_map/ppermute | solution.py:14
  158.2 20.5 %copy-start.4 = (bf16[128,4096]{1,0:T(8,128)(2,1)}, bf16[128,4096]{1,0:T(8,128)(2,1)S(1)}, u32[]{:S(2)}) copy-start(bf16[128,4096]{1,0:T(8,128)(2,1)S(1)} %collective-permute-done.1) | copy-start | bytes 3145732
  158.2 52.1 %collective-permute-start.6 = (bf16[128,4096]{1,0:T(8,128)(2,1)S(1)}, bf16[128,4096]{1,0:T(8,128)(2,1)}, u32[]{:S(2)}, u32[]{:S(2)}) collective-permute-start(bf16[128,4096]{1,0:T(8,128)(2,1)S(1)} %get-tuple-element.25), channel_id=1, source_target_pairs={{0,112},{4,116},{8,120},{12,124},{1,113},{5,117},{9,121},{13,125},... | collective-permute-start | bytes 3145736 | tf_op jit(solution)/shard_map/ppermute | solution.py:14
  216.1 21.3 %collective-permute-start.7 = (bf16[128,4096]{1,0:T(8,128)(2,1)S(1)}, bf16[128,4096]{1,0:T(8,128)(2,1)S(1)}, u32[]{:S(2)}, u32[]{:S(2)}) collective-permute-start(bf16[128,4096]{1,0:T(8,128)(2,1)S(1)} %add_convert_fusion), channel_id=1, source_target_pairs={{124,0},{0,4},{4,8},{8,12},{12,16},{16,20},{20,24},{24,28},{28,32}... | collective-permute-start | bytes 3145736 | tf_op jit(solution)/shard_map/ppermute | solution.py:20
Sparse Core Ops, SparseCore 0:
  10.8 50.6 all-gather.1
  95.5 47.1 reduce-scatter.1
where the time goes:
time: 246 us; the launch traced here: 245 us
  waiting for transfers between devices  107 us (43%)
  starting transfers between devices  68.9 us (28%)
  matrix products  33.5 us (14%)
  between operations  17.8 us (7%)
  other arithmetic  10.1 us (4%)
  local copies, waits for them, and re-layouts  7.55 us (3%)
    ppermute x7, starting transfers between devices, passed_along(): lax.ppermute(value, axis, [(source, source + steps) for source in range(f...  68.8 us
    all_gather x1, waiting for transfers between devices, on_device(): row_piece = lax.all_gather(normed, 'tensor', axis=0, tiled=True)  50.7 us
    ppermute x7, waiting for transfers between devices, passed_along(): lax.ppermute(value, axis, [(source, source + steps) for source in range(f...  35.4 us
    ppermute x1, waiting for transfers between devices, from_behind(): return lax.ppermute(block, axis, route)  21.2 us
    dot_general x1, matrix products, on_device(): jnp.dot(row_piece, query_local, preferred_element_type=jnp.float32)  7.47 us
    sub x1, matrix products, attend(): softmax_weights = jax.nn.softmax(scores, axis=-1).astype(jnp.bfloat16)  7.28 us
    dot_general x1, matrix products, attend(): jnp.einsum('gjts,sgd->tgjd', softmax_weights, value_rows, preferred_eleme...  5.99 us
    convert_element_type x1, other arithmetic, on_device(): (self_coefficient[0] * block_out.astype(jnp.float32) + history_sum).astyp...  5.81 us
  transfers between devices with their start and end apart: 10, of which 5 were waited for; matrix products, arithmetic and copies ran while one was open for 3% of the time, Pallas kernels for 0%

commit v1 on v0

--- a/solution.py
+++ b/solution.py
@@ -67,7 +67,15 @@
     query_local = query_weight[0]
     key_local = key_weight[0]
     value_local = value_weight[0]
-    row_piece = lax.all_gather(normed, "tensor", axis=0, tiled=True)
+    row_piece = jnp.concatenate(
+        jax.lax.all_to_all(
+            jnp.stack([normed for _ in range(jax.lax.axis_size("tensor"))], axis=0),
+            concat_axis=0,
+            axis_name="tensor",
+            split_axis=0,
+        ),
+        axis=0,
+    )
     query_part = jnp.dot(row_piece, query_local, preferred_element_type=jnp.float32).astype(
         jnp.bfloat16
     )

time: 246 us -> 253 us (1.028)
  starting transfers between devices: 68.9 us -> 72.7 us
    all_gather x1 -> x0, waiting for transfers between devices: 50.7 us -> none  [on_device(): row_piece = lax.all_gather(normed, 'tensor', axis=0, tiled=True)]
    all_to_all x0 -> x1, waiting for transfers between devices: none -> 48.9 us  [on_device(): jax.lax.all_to_all(jnp.stack([normed for _ in range(jax.lax.axis_size('te...]
    all_to_all x0 -> x1, starting transfers between devices: none -> 4.83 us  [on_device(): jax.lax.all_to_all(jnp.stack([normed for _ in range(jax.lax.axis_size('te...]
    dot_general x1, matrix products: 5.2 us -> 7.79 us  [on_device(): jnp.dot(row_piece, output_local, preferred_element_type=jnp.float32)]
  transfers between devices with their start and end apart: 10 -> 10, of which waited for: 5 -> 5; matrix products, arithmetic and copies ran while one was open for 3% -> 2% of each run, Pallas kernels for 0% -> 0%
where the time goes in v1:
time: 253 us
  waiting for transfers between devices  107 us (42%)
  starting transfers between devices  72.7 us (29%)
  matrix products  35.8 us (14%)
  between operations  18.1 us (7%)
  local copies, waits for them, and re-layouts  9.69 us (4%)
  other arithmetic  9.31 us (4%)
    ppermute x7, starting transfers between devices, passed_along(): lax.ppermute(value, axis, [(source, source + steps) for source in range(f...  67.8 us
    all_to_all x1, waiting for transfers between devices, on_device(): jax.lax.all_to_all(jnp.stack([normed for _ in range(jax.lax.axis_size('te...  48.9 us
    ppermute x7, waiting for transfers between devices, passed_along(): lax.ppermute(value, axis, [(source, source + steps) for source in range(f...  34.8 us
    ppermute x1, waiting for transfers between devices, from_behind(): return lax.ppermute(block, axis, route)  23.2 us
    dot_general x1, matrix products, on_device(): jnp.dot(row_piece, output_local, preferred_element_type=jnp.float32)  7.79 us
    dot_general x1, matrix products, on_device(): jnp.dot(row_piece, query_local, preferred_element_type=jnp.float32)  7.46 us
    sub x1, matrix products, attend(): softmax_weights = jax.nn.softmax(scores, axis=-1).astype(jnp.bfloat16)  7.27 us
    convert_element_type x1, other arithmetic, on_device(): (self_coefficient[0] * block_out.astype(jnp.float32) + history_sum).astyp...  6.01 us
  transfers between devices with their start and end apart: 10, of which 5 were waited for; matrix products, arithmetic and copies ran while one was open for 2% of the time, Pallas kernels for 0%

profile of v1, /device:TPU:0, one launch (start us, length us, event | category | flops | bytes accessed | tf_op | source)
XLA Modules:
  0.0 252.5 jit_solution(7688385494084288941)
XLA Ops:
  6.5 1.6 fusion.15
  8.2 1.5 fusion.24
  9.6 2.5 stack.10
  12.1 4.8 %all-to-all-start = ((bf16[4,128,4096]{2,1,0:T(8,128)(2,1)}), bf16[4,128,4096]{2,1,0:T(8,128)(2,1)}, u32[]{:S(2)}, u32[]{:S(2)}) async-start(bf16[4,128,4096]{2,1,0:T(8,128)(2,1)} %stack.10), calls=%async_computation | async-start | bytes 8388608 | tf_op jit(solution)/shard_map/all_to_all | solution.py:71
  17.0 0.0 reduce-scatter.2.cloned.1.call-start
  17.0 0.1 iota_compare_fusion
  17.1 48.9 %all-to-all-done = bf16[4,128,4096]{2,1,0:T(8,128)(2,1)} async-done(((bf16[4,128,4096]{2,1,0:T(8,128)(2,1)}), bf16[4,128,4096]{2,1,0:T(8,128)(2,1)}, u32[]{:S(2)}, u32[]{:S(2)}) %all-to-all-start) | async-done | bytes 4194336 | tf_op jit(solution)/shard_map/all_to_all | solution.py:71
  66.0 7.5 %fusion.21 = bf16[512,768]{1,0:T(8,128)(2,1)S(1)} fusion(bf16[512,4096]{1,0:T(8,128)(2,1)} %bitcast.3, bf16[1,4096,768]{2,1,0:T(8,128)(2,1)} %param.9), kind=kOutput, calls=%fused_computation.24 | convolution fusion | flops 3221618688 | bytes 11272192 | tf_op jit(solution)/shard_map/dot_general | solution.py:79
  73.5 0.3 copy.10
  73.8 3.8 %convolution_convert_fusion = bf16[512,128]{0,1:T(8,128)(2,1)S(1)} fusion(bf16[512,4096]{1,0:T(8,128)(2,1)} %bitcast.3, bf16[1,4096,128]{2,1,0:T(8,128)(2,1)S(1)} %copy-done), kind=kOutput, calls=%fused_computation.25 | convolution fusion | flops 536936448 | bytes 5373952 | tf_op jit(solution)/shard_map/dot_general | solution.py:82
  77.6 3.7 %convolution_convert_fusion.1 = bf16[512,128]{0,1:T(8,128)(2,1)S(1)} fusion(bf16[512,4096]{1,0:T(8,128)(2,1)} %bitcast.3, bf16[1,4096,128]{2,1,0:T(8,128)(2,1)S(1)} %copy-done.3), kind=kOutput, calls=%fused_computation.26 | convolution fusion | flops 536936448 | bytes 5373952 | tf_op jit(solution)/shard_map/dot_general | solution.py:85
  81.3 7.3 %fusion.30 = (f32[2,6,512]{2,1,0:T(8,128)S(1)}, f32[2,6,512,512]{2,3,1,0:T(8,128)}) fusion(pred[512,512]{0,1:T(8,128)(4,1)S(1)} %iota_compare_fusion, bf16[512,2,64,1]{0,2,3,1:T(8,128)(2,1)S(1)} %bitcast.91, bf16[512,2,6,64]{0,3,2,1:T(8,128)(2,1)S(1)} %bitcast.89), kind=kOutput, calls=%fused_computation.44 | convolution fusion | flops 415236608 | bytes 13787136 | tf_op jit(solution)/shard_map/while/body/eval_jaxpr/sub | solution.py:41
  88.6 5.8 %fusion.20 = bf16[2,64,6,512]{3,1,2,0:T(8,128)(2,1)S(1)} fusion(bf16[512,2,64,1]{0,2,3,1:T(8,128)(2,1)S(1)} %bitcast.90, f32[2,6,512,512]{2,3,1,0:T(8,128)} %get-tuple-element.36, f32[2,6,512]{2,1,0:T(8,128)S(1)} %get-tuple-element.35), kind=kOutput, calls=%fused_computation.23 | convolution fusion | flops 409337856 | bytes 13524992 | tf_op jit(solution)/shard_map/while/body/eval_jaxpr/gjts,sgd->tgjd/dot_general | solution.py:42
  94.4 7.8 %fusion.10 = bf16[512,4096]{1,0:T(8,128)(2,1)} fusion(bf16[512,768]{0,1:T(8,128)(2,1)S(1)} %bitcast.92, bf16[1,768,4096]{2,1,0:T(8,128)(2,1)} %param.12), kind=kOutput, calls=%fused_computation.13 | convolution fusion | flops 3223322624 | bytes 11272192 | tf_op jit(solution)/shard_map/dot_general | solution.py:107
  102.2 0.0 reduce-scatter.2.cloned.1.call-update
  102.2 5.2 %slice_bitcast_fusion.6 = (bf16[128,4096]{1,0:T(8,128)(2,1)S(1)}, bf16[128,4096]{1,0:T(8,128)(2,1)}, bf16[128,4096]{1,0:T(8,128)(2,1)}, bf16[128,4096]{1,0:T(8,1...) fusion(bf16[1,7,128,4096]{3,2,1,0:T(8,128)(2,1)} %param.8), kind=kLoop, calls=%fused_computation.36 | loop fusion | bytes 14680064 | tf_op jit(solution)/shard_map/squeeze | solution.py:58
  107.4 6.0 %collective-permute-start = (bf16[128,4096]{1,0:T(8,128)(2,1)S(1)}, bf16[128,4096]{1,0:T(8,128)(2,1)S(1)}, u32[]{:S(2)}, u32[]{:S(2)}) collective-permute-start(bf16[128,4096]{1,0:T(8,128)(2,1)S(1)} %get-tuple-element.13), channel_id=1, source_target_pairs={{0,16},{4,20},{8,24},{12,28},{16,32},{20,36},{24,40},{28,44},{32,4... | collective-permute-start | bytes 3145736 | tf_op jit(solution)/shard_map/ppermute | solution.py:14
  113.5 3.7 %collective-permute-start.1 = (bf16[128,4096]{1,0:T(8,128)(2,1)S(1)}, bf16[128,4096]{1,0:T(8,128)(2,1)S(1)}, u32[]{:S(2)}, u32[]{:S(2)}) collective-permute-start(bf16[128,4096]{1,0:T(8,128)(2,1)S(1)} %get-tuple-element.24), channel_id=1, source_target_pairs={{0,32},{4,36},{8,40},{12,44},{16,48},{20,52},{24,56},{28,60},{32,6... | collective-permute-start | bytes 3145736 | tf_op jit(solution)/shard_map/ppermute | solution.py:14
  117.2 4.2 %collective-permute-start.2 = (bf16[128,4096]{1,0:T(8,128)(2,1)}, bf16[128,4096]{1,0:T(8,128)(2,1)}, u32[]{:S(2)}, u32[]{:S(2)}) collective-permute-start(bf16[128,4096]{1,0:T(8,128)(2,1)} %get-tuple-element.22), channel_id=1, source_target_pairs={{0,48},{4,52},{8,56},{12,60},{16,64},{20,68},{24,72},{28,76},{32,8... | collective-permute-start | bytes 3145736 | tf_op jit(solution)/shard_map/ppermute | solution.py:14
  121.3 3.5 %collective-permute-start.3 = (bf16[128,4096]{1,0:T(8,128)(2,1)}, bf16[128,4096]{1,0:T(8,128)(2,1)}, u32[]{:S(2)}, u32[]{:S(2)}) collective-permute-start(bf16[128,4096]{1,0:T(8,128)(2,1)} %get-tuple-element.20), channel_id=1, source_target_pairs={{0,64},{4,68},{8,72},{12,76},{16,80},{20,84},{24,88},{28,92},{32,9... | collective-permute-start | bytes 3145736 | tf_op jit(solution)/shard_map/ppermute | solution.py:14
  124.9 2.3 collective-permute-start.4
  127.2 7.8 %collective-permute-done = bf16[128,4096]{1,0:T(8,128)(2,1)S(1)} collective-permute-done((bf16[128,4096]{1,0:T(8,128)(2,1)S(1)}, bf16[128,4096]{1,0:T(8,128)(2,1)S(1)}, u32[]{:S(2)}, u32[]{:S(2)}) %collective-permute-start) | collective-permute-done | bytes 1048608 | tf_op jit(solution)/shard_map/ppermute | solution.py:14
  135.0 28.7 %collective-permute-start.5 = (bf16[128,4096]{1,0:T(8,128)(2,1)S(1)}, bf16[128,4096]{1,0:T(8,128)(2,1)}, u32[]{:S(2)}, u32[]{:S(2)}) collective-permute-start(bf16[128,4096]{1,0:T(8,128)(2,1)S(1)} %get-tuple-element.26), channel_id=1, source_target_pairs={{0,96},{4,100},{8,104},{12,108},{16,112},{20,116},{24,120},{28,124... | collective-permute-start | bytes 3145736 | tf_op jit(solution)/shard_map/ppermute | solution.py:14
  163.7 19.3 %collective-permute-start.6 = (bf16[128,4096]{1,0:T(8,128)(2,1)S(1)}, bf16[128,4096]{1,0:T(8,128)(2,1)}, u32[]{:S(2)}, u32[]{:S(2)}) collective-permute-start(bf16[128,4096]{1,0:T(8,128)(2,1)S(1)} %get-tuple-element.25), channel_id=1, source_target_pairs={{0,112},{4,116},{8,120},{12,124},{1,113},{5,117},{9,121},{13,125},... | collective-permute-start | bytes 3145736 | tf_op jit(solution)/shard_map/ppermute | solution.py:14
  183.0 0.1 multiply_reduce_fusion
  183.1 0.7 fusion.29
  188.4 17.4 %collective-permute-done.4 = bf16[128,4096]{1,0:T(8,128)(2,1)} collective-permute-done((bf16[128,4096]{1,0:T(8,128)(2,1)}, bf16[128,4096]{1,0:T(8,128)(2,1)}, u32[]{:S(2)}, u32[]{:S(2)}) %collective-permute-start.4) | collective-permute-done | bytes 1048608 | tf_op jit(solution)/shard_map/ppermute | solution.py:14
  205.8 9.6 %collective-permute-done.6 = bf16[128,4096]{1,0:T(8,128)(2,1)} collective-permute-done((bf16[128,4096]{1,0:T(8,128)(2,1)S(1)}, bf16[128,4096]{1,0:T(8,128)(2,1)}, u32[]{:S(2)}, u32[]{:S(2)}) %collective-permute-start.6) | collective-permute-done | bytes 1048608 | tf_op jit(solution)/shard_map/ppermute | solution.py:14
  215.4 6.0 %add_convert_fusion = bf16[128,4096]{1,0:T(8,128)(2,1)S(1)} fusion(bf16[128,4096]{1,0:T(8,128)(2,1)} %collective-permute-done.6, bf16[128,4096]{1,0:T(8,128)(2,1)} %collective-permute-done.5, bf16[128,4096]{1,0:T(8,128)(2,1)} %collective-permute-done.4, bf16[128,4096]{1,0:T(8,128)(2,1)} %collective-permute-done.3, ...), kind=kLoop, calls=%fused_computation.21 | loop fusion | flops 14680064 | bytes 10485792 | tf_op jit(solution)/shard_map/convert_element_type | solution.py:117
  221.4 0.1 collective-permute-start.7
  221.5 23.2 %collective-permute-done.7 = bf16[128,4096]{1,0:T(8,128)(2,1)S(1)} collective-permute-done((bf16[128,4096]{1,0:T(8,128)(2,1)S(1)}, bf16[128,4096]{1,0:T(8,128)(2,1)S(1)}, u32[]{:S(2)}, u32[]{:S(2)}) %collective-permute-start.7) | collective-permute-done | bytes 1048608 | tf_op jit(solution)/shard_map/ppermute | solution.py:20
  244.7 1.0 copy.16
  (21 shorter events, 0.1 us)
Async XLA Ops:
  6.5 67.3 %copy-start = (bf16[1,4096,128]{2,1,0:T(8,128)(2,1)S(1)}, bf16[1,4096,128]{2,1,0:T(8,128)(2,1)}, u32[]{:S(2)}) copy-start(bf16[1,4096,128]{2,1,0:T(8,128)(2,1)} %param.10) | copy-start | bytes 3145732
  12.1 53.9 %all-to-all-start = ((bf16[4,128,4096]{2,1,0:T(8,128)(2,1)}), bf16[4,128,4096]{2,1,0:T(8,128)(2,1)}, u32[]{:S(2)}, u32[]{:S(2)}) async-start(bf16[4,128,4096]{2,1,0:T(8,128)(2,1)} %stack.10), calls=%async_computation | async-start | bytes 8388608 | tf_op jit(solution)/shard_map/all_to_all | solution.py:71
  17.0 198.4 %reduce-scatter.2.cloned.1.call-start = ((), (), s32[]{:S(2)}) async-start(), calls=%async_computation.2 | async-start | bytes 5242880 | tf_op jit(solution)/shard_map/reduce_scatter | solution.py:110
  73.8 3.8 %copy-start.3 = (bf16[1,4096,128]{2,1,0:T(8,128)(2,1)S(1)}, bf16[1,4096,128]{2,1,0:T(8,128)(2,1)}, u32[]{:S(2)}) copy-start(bf16[1,4096,128]{2,1,0:T(8,128)(2,1)} %param.11) | copy-start | bytes 3145732
  102.2 80.8 %copy-start.6 = (f32[32,8]{0,1:T(8,128)S(1)}, f32[32,8]{0,1:T(8,128)}, u32[]{:S(2)}) copy-start(f32[32,8]{0,1:T(8,128)} %param.13) | copy-start | bytes 3076
  102.2 113.2 %copy-start.2 = (bf16[1,128,4096]{2,1,0:T(8,128)(2,1)S(1)}, bf16[1,128,4096]{2,1,0:T(8,128)(2,1)}, u32[]{:S(2)}) copy-start(bf16[1,128,4096]{2,1,0:T(8,128)(2,1)} %param.7) | copy-start | bytes 3145732
  107.4 27.5 %collective-permute-start = (bf16[128,4096]{1,0:T(8,128)(2,1)S(1)}, bf16[128,4096]{1,0:T(8,128)(2,1)S(1)}, u32[]{:S(2)}, u32[]{:S(2)}) collective-permute-start(bf16[128,4096]{1,0:T(8,128)(2,1)S(1)} %get-tuple-element.13), channel_id=1, source_target_pairs={{0,16},{4,20},{8,24},{12,28},{16,32},{20,36},{24,40},{28,44},{32,4... | collective-permute-start | bytes 3145736 | tf_op jit(solution)/shard_map/ppermute | solution.py:14
  113.5 50.2 %collective-permute-start.1 = (bf16[128,4096]{1,0:T(8,128)(2,1)S(1)}, bf16[128,4096]{1,0:T(8,128)(2,1)S(1)}, u32[]{:S(2)}, u32[]{:S(2)}) collective-permute-start(bf16[128,4096]{1,0:T(8,128)(2,1)S(1)} %get-tuple-element.24), channel_id=1, source_target_pairs={{0,32},{4,36},{8,40},{12,44},{16,48},{20,52},{24,56},{28,60},{32,6... | collective-permute-start | bytes 3145736 | tf_op jit(solution)/shard_map/ppermute | solution.py:14
  117.2 71.2 %collective-permute-start.2 = (bf16[128,4096]{1,0:T(8,128)(2,1)}, bf16[128,4096]{1,0:T(8,128)(2,1)}, u32[]{:S(2)}, u32[]{:S(2)}) collective-permute-start(bf16[128,4096]{1,0:T(8,128)(2,1)} %get-tuple-element.22), channel_id=1, source_target_pairs={{0,48},{4,52},{8,56},{12,60},{16,64},{20,68},{24,72},{28,76},{32,8... | collective-permute-start | bytes 3145736 | tf_op jit(solution)/shard_map/ppermute | solution.py:14
  121.3 67.1 %collective-permute-start.3 = (bf16[128,4096]{1,0:T(8,128)(2,1)}, bf16[128,4096]{1,0:T(8,128)(2,1)}, u32[]{:S(2)}, u32[]{:S(2)}) collective-permute-start(bf16[128,4096]{1,0:T(8,128)(2,1)} %get-tuple-element.20), channel_id=1, source_target_pairs={{0,64},{4,68},{8,72},{12,76},{16,80},{20,84},{24,88},{28,92},{32,9... | collective-permute-start | bytes 3145736 | tf_op jit(solution)/shard_map/ppermute | solution.py:14
  124.9 80.9 %collective-permute-start.4 = (bf16[128,4096]{1,0:T(8,128)(2,1)}, bf16[128,4096]{1,0:T(8,128)(2,1)}, u32[]{:S(2)}, u32[]{:S(2)}) collective-permute-start(bf16[128,4096]{1,0:T(8,128)(2,1)} %get-tuple-element.14), channel_id=1, source_target_pairs={{0,80},{4,84},{8,88},{12,92},{16,96},{20,100},{24,104},{28,108},{3... | collective-permute-start | bytes 3145736 | tf_op jit(solution)/shard_map/ppermute | solution.py:14
  135.0 48.0 %copy-start.4 = (bf16[128,4096]{1,0:T(8,128)(2,1)}, bf16[128,4096]{1,0:T(8,128)(2,1)S(1)}, u32[]{:S(2)}) copy-start(bf16[128,4096]{1,0:T(8,128)(2,1)S(1)} %collective-permute-done) | copy-start | bytes 3145732
  135.0 70.8 %collective-permute-start.5 = (bf16[128,4096]{1,0:T(8,128)(2,1)S(1)}, bf16[128,4096]{1,0:T(8,128)(2,1)}, u32[]{:S(2)}, u32[]{:S(2)}) collective-permute-start(bf16[128,4096]{1,0:T(8,128)(2,1)S(1)} %get-tuple-element.26), channel_id=1, source_target_pairs={{0,96},{4,100},{8,104},{12,108},{16,112},{20,116},{24,120},{28,124... | collective-permute-start | bytes 3145736 | tf_op jit(solution)/shard_map/ppermute | solution.py:14
  163.7 19.3 %copy-start.5 = (bf16[128,4096]{1,0:T(8,128)(2,1)}, bf16[128,4096]{1,0:T(8,128)(2,1)S(1)}, u32[]{:S(2)}) copy-start(bf16[128,4096]{1,0:T(8,128)(2,1)S(1)} %collective-permute-done.1) | copy-start | bytes 3145732
  163.7 51.7 %collective-permute-start.6 = (bf16[128,4096]{1,0:T(8,128)(2,1)S(1)}, bf16[128,4096]{1,0:T(8,128)(2,1)}, u32[]{:S(2)}, u32[]{:S(2)}) collective-permute-start(bf16[128,4096]{1,0:T(8,128)(2,1)S(1)} %get-tuple-element.25), channel_id=1, source_target_pairs={{0,112},{4,116},{8,120},{12,124},{1,113},{5,117},{9,121},{13,125},... | collective-permute-start | bytes 3145736 | tf_op jit(solution)/shard_map/ppermute | solution.py:14
  215.4 30.3 %copy-start.1 = (bf16[1,4096,128]{2,1,0:T(8,128)(2,1)S(1)}, bf16[1,4096,128]{2,1,0:T(8,128)(2,1)}, u32[]{:S(2)}) copy-start(bf16[1,4096,128]{2,1,0:T(8,128)(2,1)} %param.10) | copy-start | bytes 3145732
  221.4 23.3 %collective-permute-start.7 = (bf16[128,4096]{1,0:T(8,128)(2,1)S(1)}, bf16[128,4096]{1,0:T(8,128)(2,1)S(1)}, u32[]{:S(2)}, u32[]{:S(2)}) collective-permute-start(bf16[128,4096]{1,0:T(8,128)(2,1)S(1)} %add_convert_fusion), channel_id=1, source_target_pairs={{124,0},{0,4},{4,8},{8,12},{12,16},{16,20},{20,24},{24,28},{28,32}... | collective-permute-start | bytes 3145736 | tf_op jit(solution)/shard_map/ppermute | solution.py:20
Sparse Core Ops, SparseCore 0:
  102.3 47.4 reduce-scatter.1
